TPU v7x, 32 devices: a whole 2x2x4 slice. The times are simulated.
32 devices in a mesh: dp: 2 (over x), crop: 4 (over y, core), tensor: 4 (over z).
Axes of the slice: x: 2, y: 2, z: 4, core: 2. Of those that a mesh axis runs over, the one named last changes fastest.
Arguments:
- hidden_a: bfloat16 [512, 8192], P('crop', 'dp'), as said below
- hidden_b: bfloat16 [512, 8192], P('crop', 'dp'), as said below
- weight: bfloat16 [8192, 8192], P('dp', 'tensor')
Outputs:
- weight_grad: float32 [8192, 8192], P(('dp', 'crop'), 'tensor')
Inputs may be any that keep to these rules, and one draw needn't show every extreme that they name: `hidden_a`: nonnegative entries. `hidden_b`: nonnegative entries.
All inputs are finite; a program needn't handle non-finite values.
Results may differ from a plain program's by a relative error of at most 0.0015.
Values may be sent and summed in bfloat16 or wider, within the bound.
A program may use at most 128 MiB of HBM per device.

v0:
```python
import jax
import jax.numpy as jnp
from jax import lax
from jax.sharding import PartitionSpec as P

epsilon = 0.0001


def body(hidden_a, hidden_b, weight):
    group_size = lax.axis_size(("dp", "crop"))
    data_count = lax.axis_size("dp")
    block_rows = hidden_a.shape[0]
    local_rows = block_rows // data_count
    total_rows = local_rows * group_size
    left_part = jnp.dot(hidden_a, weight, preferred_element_type=jnp.float32)
    right_part = jnp.dot(hidden_b, weight, preferred_element_type=jnp.float32)
    joined = lax.psum_scatter(
        jnp.stack([left_part, right_part], axis=1), "dp", scatter_dimension=0, tiled=True
    ).astype(jnp.bfloat16)
    stacked = jnp.stack([joined[:, 0, :], joined[:, 1, :]]).astype(jnp.float32)
    col_means = lax.psum(jnp.sum(stacked, axis=1), ("dp", "crop")) / total_rows
    centered = stacked - col_means[:, None, :]
    spread = lax.psum(jnp.sum(centered * centered, axis=1), ("dp", "crop"))
    deviation = jnp.sqrt(spread / (total_rows - 1.0) + epsilon)
    rounded = centered.astype(jnp.bfloat16)
    everyone = lax.all_gather(rounded, ("dp", "crop"), axis=1, tiled=True)
    gram = jnp.einsum("vrf,vbf->vrb", rounded, everyone, preferred_element_type=jnp.float32)
    gram = lax.psum(gram, "tensor")
    gram_low = gram.astype(jnp.bfloat16)
    products = jnp.einsum("vrb,vbf->vrf", gram_low, everyone, preferred_element_type=jnp.float32)
    hinge_rate = jnp.where(deviation < 1.0, 25.0 / ((total_rows - 1.0) * deviation), 0.0)[
        :, None, :
    ]
    differ = stacked[0] - stacked[1]
    pull_term = jnp.stack([differ, -differ]) * (50.0 / total_rows)
    cov_scale = 4.0 / (total_rows - 1.0) ** 2
    row_grads = (
        pull_term - hinge_rate * centered + cov_scale * (products - centered * spread[:, None, :])
    )
    row_grads = row_grads.astype(jnp.bfloat16)
    block_grads = lax.all_gather(row_grads, "dp", axis=1, tiled=True)
    across = (((0,), (0,)), ((), ()))
    left_part = lax.dot_general(
        hidden_a, block_grads[0], across, preferred_element_type=jnp.float32
    )
    right_part = lax.dot_general(
        hidden_b, block_grads[1], across, preferred_element_type=jnp.float32
    )
    return lax.psum_scatter(left_part + right_part, "crop", scatter_dimension=0, tiled=True)


def solution(mesh):
    placed = (P("crop", "dp"), P("crop", "dp"), P("dp", "tensor"))
    return jax.shard_map(
        body, mesh=mesh, in_specs=placed, out_specs=P(("dp", "crop"), "tensor"), check_vma=False
    )
```

profile of v0, /device:TPU:0, one launch (start us, length us, event | category | flops | bytes accessed | tf_op | source)
XLA Modules:
  0.0 458.1 jit_solution(6418926525455714938)
XLA Ops:
  6.5 1.2 copy-done
  7.8 8.2 %convolution_bitcast_fusion.1 = f32[128,1,2048]{2,0,1:T(8,128)S(1)} fusion(bf16[128,4096]{1,0:T(8,128)(2,1)S(1)} %copy-done, bf16[4096,2048]{1,0:T(8,128)(2,1)} %param.5), kind=kOutput, calls=%fused_computation.5 | convolution fusion | flops 2147483648 | bytes 18874368 | tf_op jit(solution)/shard_map/dot_general | solution.py:15
  16.0 2.4 copy-done.2
  18.4 2.4 convolution_bitcast_fusion
  20.8 1.5 pad_maximum_fusion
  22.3 34.7 %reduce-scatter.3.cloned.1.call-done = f32[64,2,2048]{2,0,1:T(8,128)} async-done(((f32[128,2,2048]{2,0,1:T(8,128)}), f32[64,2,2048]{2,0,1:T(8,128)}) %reduce-scatter.3.cloned.1.call-update) | async-done | bytes 1048592 | tf_op jit(solution)/shard_map/reduce_scatter | solution.py:17
  57.1 1.3 convert_element_type.15
  58.4 0.1 convert_reduce_fusion
  58.5 22.9 %psum.21 = f32[2,2048]{1,0:T(2,128)S(1)} all-reduce(f32[2,2048]{1,0:T(2,128)S(1)} %convert_reduce_fusion), channel_id=1, replica_groups=mesh['dp'=2,'crop'=4,'tensor'=4] {'dp','crop'}, use_global_device_ids=true, to_apply=%region_2.0 | all-reduce | flops 4096 | bytes 32768 | tf_op jit(solution)/shard_map/psum | solution.py:21
  81.5 1.0 multiply_reduce_fusion
  82.5 22.7 %psum.22 = f32[2,2048]{1,0:T(2,128)S(1)} all-reduce(f32[2,2048]{1,0:T(2,128)S(1)} %get-tuple-element.7), channel_id=1, replica_groups=mesh['dp'=2,'crop'=4,'tensor'=4] {'dp','crop'}, use_global_device_ids=true, to_apply=%region_4.0 | all-reduce | flops 4096 | bytes 32768 | tf_op jit(solution)/shard_map/psum | solution.py:23
  105.3 0.5 copy-done.5
  105.8 0.6 compare_select_fusion
  106.4 0.9 fusion.7
  107.3 12.0 %all-gather.3.cloned.1.call-done = bf16[2,512,2048]{2,1,0:T(8,128)(2,1)} async-done(((bf16[2,64,2048]{2,1,0:T(8,128)(2,1)}), bf16[2,512,2048]{2,1,0:T(8,128)(2,1)}) %all-gather.3.cloned.1.call-update) | async-done | bytes 4194320 | tf_op jit(solution)/shard_map/all_gather | solution.py:26
  119.3 3.7 fusion.8
  123.1 24.7 %all-reduce.1 = bf16[2,64,512]{2,1,0:T(8,128)(2,1)S(1)} all-reduce(f32[2,64,512]{2,1,0:T(8,128)S(1)} %fusion.8), channel_id=1, replica_groups=mesh['dp'=2,'crop'=4,'tensor'=4] {'tensor'}, use_global_device_ids=true, to_apply=%region_5.0 | all-reduce | flops 65536 | bytes 393216 | tf_op jit(solution)/shard_map/psum | solution.py:28
  147.7 4.2 fusion.2
  152.0 0.2 reduce-scatter.5.cloned.1.call-start
  152.2 18.8 %all-gather.5.cloned.1.call-done = bf16[2,128,2048]{2,1,0:T(8,128)(2,1)} async-done(((bf16[2,64,2048]{2,1,0:T(8,128)(2,1)}), bf16[2,128,2048]{2,1,0:T(8,128)(2,1)}) %all-gather.5.cloned.1.call-update) | async-done | bytes 1048592 | tf_op jit(solution)/shard_map/all_gather | solution.py:41
  171.0 14.3 %fusion.4 = f32[2048,4096]{1,0:T(8,128)} fusion(bf16[128,4096]{1,0:T(8,128)(2,1)S(1)} %copy-done, bf16[2,128,2048]{2,1,0:T(8,128)(2,1)} %all-gather.5.cloned.1.call-done), kind=kOutput, calls=%fused_computation.15 | convolution fusion | flops 2147483648 | bytes 35127296 | tf_op jit(solution)/shard_map/dot_general | solution.py:43
  185.3 24.8 %add_bitcast_fusion = f32[4096,2048]{0,1:T(8,128)} fusion(f32[2048,4096]{1,0:T(8,128)} %fusion.4, bf16[128,4096]{1,0:T(8,128)(2,1)S(1)} %copy-done.3, bf16[2,128,2048]{2,1,0:T(8,128)(2,1)S(1)} %copy-done.4), kind=kOutput, calls=%fused_computation | convolution fusion | flops 2155872256 | bytes 68681728 | tf_op jit(solution)/shard_map/dot_general | solution.py:46
  210.1 232.3 %reduce-scatter.5.cloned.1.call-done = f32[1024,2048]{0,1:T(8,128)} async-done(((f32[4096,2048]{0,1:T(8,128)}), f32[1024,2048]{0,1:T(8,128)}) %reduce-scatter.5.cloned.1.call-update) | async-done | bytes 8388624 | tf_op jit(solution)/shard_map/reduce_scatter | solution.py:49
  442.4 9.1 %copy.4 = f32[1024,2048]{1,0:T(8,128)} copy(f32[1024,2048]{0,1:T(8,128)} %reduce-scatter.5.cloned.1.call-done) | data formatting | bytes 16777216 | tf_op jit(solution)/shard_map/reduce_scatter | solution.py:49
  (19 shorter events, 0.3 us)
Async XLA Ops:
  6.5 1.2 copy-start
  6.5 9.5 %copy-start.3 = (bf16[128,4096]{1,0:T(8,128)(2,1)S(1)}, bf16[128,4096]{1,0:T(8,128)(2,1)}, u32[]{:S(2)}) copy-start(bf16[128,4096]{1,0:T(8,128)(2,1)} %param.4) | copy-start | bytes 3145732
  6.5 50.5 %reduce-scatter.3.cloned.1.call-start = ((), (), s32[]{:S(2)}) async-start(), calls=%async_computation.2 | async-start | bytes 3145728 | tf_op jit(solution)/shard_map/reduce_scatter | solution.py:17
  7.8 10.6 %copy-start.2 = (bf16[4096,2048]{1,0:T(8,128)(2,1)S(1)}, bf16[4096,2048]{1,0:T(8,128)(2,1)}, u32[]{:S(2)}) copy-start(bf16[4096,2048]{1,0:T(8,128)(2,1)} %param.5) | copy-start | bytes 50331652
  22.3 97.0 %all-gather.3.cloned.1.call-start = ((), (), s32[]{:S(2)}) async-start(), calls=%async_computation.3 | async-start | bytes 4718592 | tf_op jit(solution)/shard_map/all_gather | solution.py:26
  82.4 88.5 %all-gather.5.cloned.1.call-start = ((), (), s32[]{:S(2)}) async-start(), calls=%async_computation.4 | async-start | bytes 1572864 | tf_op jit(solution)/shard_map/all_gather | solution.py:41
  105.2 0.6 copy-start.5
  152.0 290.4 %reduce-scatter.5.cloned.1.call-start = ((), (), s32[]{:S(2)}) async-start(), calls=%async_computation.5 | async-start | bytes 41943040 | tf_op jit(solution)/shard_map/reduce_scatter | solution.py:49
  171.0 14.3 %copy-start.4 = (bf16[2,128,2048]{2,1,0:T(8,128)(2,1)S(1)}, bf16[2,128,2048]{2,1,0:T(8,128)(2,1)}, u32[]{:S(2)}) copy-start(bf16[2,128,2048]{2,1,0:T(8,128)(2,1)} %all-gather.5.cloned.1.call-done) | copy-start | bytes 3145732
  210.1 241.5 %copy-start.1 = (bf16[128,4096]{1,0:T(8,128)(2,1)S(1)}, bf16[128,4096]{1,0:T(8,128)(2,1)}, u32[]{:S(2)}) copy-start(bf16[128,4096]{1,0:T(8,128)(2,1)} %param.3) | copy-start | bytes 3145732
Sparse Core Ops, SparseCore 0:
  22.4 34.6 reduce-scatter.2
  82.6 36.6 all-gather.2
  152.1 18.8 all-gather.4
  210.2 232.1 reduce-scatter.4
where the time goes:
time: 458 us
  waiting for transfers between devices  298 us (65%)
  blocking collectives  70.3 us (15%)
  matrix products  57.7 us (13%)
  local copies, waits for them, and re-layouts  13.3 us (3%)
  between operations  13.2 us (3%)
  other arithmetic  5.43 us (1%)
    reduce_scatter x1, waiting for transfers between devices, body(): lax.psum_scatter(left_part + right_part, 'crop', scatter_dimension=0, til...  232 us
    reduce_scatter x1, waiting for transfers between devices, body(): lax.psum_scatter(jnp.stack([left_part, right_part], axis=1), 'dp', scatte...  34.7 us
    dot_general x1, matrix products, body(): lax.dot_general(hidden_b, block_grads[1], across, preferred_element_type=...  24.8 us
    psum x1, blocking collectives, body(): gram = lax.psum(gram, 'tensor')  24.7 us
    psum x1, blocking collectives, body(): col_means = lax.psum(jnp.sum(stacked, axis=1), ('dp', 'crop')) / total_rows  22.9 us
    psum x1, blocking collectives, body(): spread = lax.psum(jnp.sum(centered * centered, axis=1), ('dp', 'crop'))  22.7 us
    all_gather x1, waiting for transfers between devices, body(): block_grads = lax.all_gather(row_grads, 'dp', axis=1, tiled=True)  18.8 us
    dot_general x1, matrix products, body(): lax.dot_general(hidden_a, block_grads[0], across, preferred_element_type=...  14.3 us
  transfers between devices with their start and end apart: 4, of which 4 were waited for; matrix products, arithmetic and copies ran while one was open for 0% of the time, Pallas kernels for 0%

commit v1 on v0

--- a/solution.py
+++ b/solution.py
@@ -25,7 +25,8 @@
     rounded = centered.astype(jnp.bfloat16)
     everyone = lax.all_gather(rounded, ("dp", "crop"), axis=1, tiled=True)
     gram = jnp.einsum("vrf,vbf->vrb", rounded, everyone, preferred_element_type=jnp.float32)
-    gram = lax.psum(gram, "tensor")
+    space_return_all = lambda packet: jnp.sum(lax.all_gather(packet, axis_name="tensor"), axis=0)
+    gram = space_return_all(gram)
     gram_low = gram.astype(jnp.bfloat16)
     products = jnp.einsum("vrb,vbf->vrf", gram_low, everyone, preferred_element_type=jnp.float32)
     hinge_rate = jnp.where(deviation < 1.0, 25.0 / ((total_rows - 1.0) * deviation), 0.0)[

time: 458 us -> 466 us (1.017)
  waiting for transfers between devices: 298 us -> 327 us
  blocking collectives: 70.3 us -> 47.2 us
    all_gather x1, waiting for transfers between devices: 12 us -> 36.7 us  [body(): everyone = lax.all_gather(rounded, ('dp', 'crop'), axis=1, tiled=True)]
    psum x1 -> x0, blocking collectives: 24.7 us -> none  [body(): gram = lax.psum(gram, 'tensor')]
  transfers between devices with their start and end apart: 4 -> 5, of which waited for: 4 -> 5; matrix products, arithmetic and copies ran while one was open for 0% -> 0% of each run, Pallas kernels for 0% -> 0%
where the time goes in v1:
time: 466 us; the launch traced here: 465 us
  waiting for transfers between devices  327 us (70%)
  matrix products  58.3 us (13%)
  blocking collectives  47.2 us (10%)
  between operations  13.2 us (3%)
  local copies, waits for them, and re-layouts  12.7 us (3%)
  other arithmetic  6.17 us (1%)
    reduce_scatter x1, waiting for transfers between devices, body(): lax.psum_scatter(left_part + right_part, 'crop', scatter_dimension=0, til...  232 us
    all_gather x1, waiting for transfers between devices, body(): everyone = lax.all_gather(rounded, ('dp', 'crop'), axis=1, tiled=True)  36.7 us
    reduce_scatter x1, waiting for transfers between devices, body(): lax.psum_scatter(jnp.stack([left_part, right_part], axis=1), 'dp', scatte...  34.7 us
    dot_general x1, matrix products, body(): lax.dot_general(hidden_b, block_grads[1], across, preferred_element_type=...  24.7 us
    psum x1, blocking collectives, body(): spread = lax.psum(jnp.sum(centered * centered, axis=1), ('dp', 'crop'))  24.3 us
    psum x1, blocking collectives, body(): col_means = lax.psum(jnp.sum(stacked, axis=1), ('dp', 'crop')) / total_rows  22.9 us
    all_gather x1, waiting for transfers between devices, body(): block_grads = lax.all_gather(row_grads, 'dp', axis=1, tiled=True)  20.6 us
    dot_general x1, matrix products, body(): lax.dot_general(hidden_a, block_grads[0], across, preferred_element_type=...  14.3 us
  transfers between devices with their start and end apart: 5, of which 5 were waited for; matrix products, arithmetic and copies ran while one was open for 0% of the time, Pallas kernels for 0%

profile of v1, /device:TPU:0, one launch (start us, length us, event | category | flops | bytes accessed | tf_op | source)
XLA Modules:
  0.0 465.1 jit_solution(1923657754421302038)
XLA Ops:
  6.5 1.2 copy-done
  7.8 8.2 %convolution_bitcast_fusion.1 = f32[128,1,2048]{2,0,1:T(8,128)S(1)} fusion(bf16[128,4096]{1,0:T(8,128)(2,1)S(1)} %copy-done, bf16[4096,2048]{1,0:T(8,128)(2,1)} %param.5), kind=kOutput, calls=%fused_computation.5 | convolution fusion | flops 2147483648 | bytes 18874368 | tf_op jit(solution)/shard_map/dot_general | solution.py:15
  16.0 2.4 copy-done.2
  18.4 2.4 convolution_bitcast_fusion
  20.8 1.5 pad_maximum_fusion
  22.3 34.7 %reduce-scatter.3.cloned.1.call-done = f32[64,2,2048]{2,0,1:T(8,128)} async-done(((f32[128,2,2048]{2,0,1:T(8,128)}), f32[64,2,2048]{2,0,1:T(8,128)}) %reduce-scatter.3.cloned.1.call-update) | async-done | bytes 1048592 | tf_op jit(solution)/shard_map/reduce_scatter | solution.py:17
  57.1 1.3 convert_element_type.15
  58.4 0.1 convert_reduce_fusion
  58.5 22.9 %psum.14 = f32[2,2048]{1,0:T(2,128)S(1)} all-reduce(f32[2,2048]{1,0:T(2,128)S(1)} %convert_reduce_fusion), channel_id=1, replica_groups=mesh['dp'=2,'crop'=4,'tensor'=4] {'dp','crop'}, use_global_device_ids=true, to_apply=%region_2.0 | all-reduce | flops 4096 | bytes 32768 | tf_op jit(solution)/shard_map/psum | solution.py:21
  81.5 1.0 multiply_reduce_fusion
  82.5 36.7 %all-gather.5.cloned.1.call-done = bf16[2,512,2048]{2,1,0:T(8,128)(2,1)} async-done(((bf16[2,64,2048]{2,1,0:T(8,128)(2,1)}), bf16[2,512,2048]{2,1,0:T(8,128)(2,1)}) %all-gather.5.cloned.1.call-update) | async-done | bytes 4194320 | tf_op jit(solution)/shard_map/all_gather | solution.py:26
  119.2 4.5 fusion.8
  123.7 24.3 %psum.15 = f32[2,2048]{1,0:T(2,128)S(1)} all-reduce(f32[2,2048]{1,0:T(2,128)S(1)} %get-tuple-element.7), channel_id=1, replica_groups=mesh['dp'=2,'crop'=4,'tensor'=4] {'dp','crop'}, use_global_device_ids=true, to_apply=%region_4.0 | all-reduce | flops 4096 | bytes 32768 | tf_op jit(solution)/shard_map/psum | solution.py:23
  148.0 0.1 fusion.6
  148.1 0.9 fusion.7
  149.0 2.8 all-gather.9.cloned.1.call-done
  151.8 1.3 reduce_sum.29
  153.1 4.2 fusion.2
  157.3 0.2 reduce-scatter.5.cloned.1.call-start
  157.5 20.6 %all-gather.7.cloned.1.call-done = bf16[2,128,2048]{2,1,0:T(8,128)(2,1)} async-done(((bf16[2,64,2048]{2,1,0:T(8,128)(2,1)}), bf16[2,128,2048]{2,1,0:T(8,128)(2,1)}) %all-gather.7.cloned.1.call-update) | async-done | bytes 1048592 | tf_op jit(solution)/shard_map/all_gather | solution.py:42
  178.1 14.3 %fusion.4 = f32[2048,4096]{1,0:T(8,128)} fusion(bf16[128,4096]{1,0:T(8,128)(2,1)S(1)} %copy-done, bf16[2,128,2048]{2,1,0:T(8,128)(2,1)} %all-gather.7.cloned.1.call-done), kind=kOutput, calls=%fused_computation.15 | convolution fusion | flops 2147483648 | bytes 35127296 | tf_op jit(solution)/shard_map/dot_general | solution.py:44
  192.4 24.7 %add_bitcast_fusion = f32[4096,2048]{0,1:T(8,128)} fusion(f32[2048,4096]{1,0:T(8,128)} %fusion.4, bf16[128,4096]{1,0:T(8,128)(2,1)S(1)} %copy-done.3, bf16[2,128,2048]{2,1,0:T(8,128)(2,1)S(1)} %copy-done.4), kind=kOutput, calls=%fused_computation | convolution fusion | flops 2155872256 | bytes 68681728 | tf_op jit(solution)/shard_map/dot_general | solution.py:47
  217.2 232.3 %reduce-scatter.5.cloned.1.call-done = f32[1024,2048]{0,1:T(8,128)} async-done(((f32[4096,2048]{0,1:T(8,128)}), f32[1024,2048]{0,1:T(8,128)}) %reduce-scatter.5.cloned.1.call-update) | async-done | bytes 8388624 | tf_op jit(solution)/shard_map/reduce_scatter | solution.py:50
  449.5 9.1 %copy.5 = f32[1024,2048]{1,0:T(8,128)} copy(f32[1024,2048]{0,1:T(8,128)} %reduce-scatter.5.cloned.1.call-done) | data formatting | bytes 16777216 | tf_op jit(solution)/shard_map/reduce_scatter | solution.py:50
  (20 shorter events, 0.3 us)
Async XLA Ops:
  6.5 1.2 copy-start
  6.5 9.5 %copy-start.3 = (bf16[128,4096]{1,0:T(8,128)(2,1)S(1)}, bf16[128,4096]{1,0:T(8,128)(2,1)}, u32[]{:S(2)}) copy-start(bf16[128,4096]{1,0:T(8,128)(2,1)} %param.4) | copy-start | bytes 3145732
  6.5 50.5 %reduce-scatter.3.cloned.1.call-start = ((), (), s32[]{:S(2)}) async-start(), calls=%async_computation.2 | async-start | bytes 3145728 | tf_op jit(solution)/shard_map/reduce_scatter | solution.py:17
  7.8 10.6 %copy-start.2 = (bf16[4096,2048]{1,0:T(8,128)(2,1)S(1)}, bf16[4096,2048]{1,0:T(8,128)(2,1)}, u32[]{:S(2)}) copy-start(bf16[4096,2048]{1,0:T(8,128)(2,1)} %param.5) | copy-start | bytes 50331652
  22.3 96.9 %all-gather.5.cloned.1.call-start = ((), (), s32[]{:S(2)}) async-start(), calls=%async_computation.3 | async-start | bytes 4718592 | tf_op jit(solution)/shard_map/all_gather | solution.py:26
  82.4 69.3 %all-gather.9.cloned.1.call-start = ((), (), s32[]{:S(2)}) async-start(), calls=%async_computation.6 | async-start | bytes 1310720 | tf_op jit(solution)/shard_map/all_gather | solution.py:28
  123.7 54.5 %all-gather.7.cloned.1.call-start = ((), (), s32[]{:S(2)}) async-start(), calls=%async_computation.4 | async-start | bytes 1572864 | tf_op jit(solution)/shard_map/all_gather | solution.py:42
  157.3 292.2 %reduce-scatter.5.cloned.1.call-start = ((), (), s32[]{:S(2)}) async-start(), calls=%async_computation.5 | async-start | bytes 41943040 | tf_op jit(solution)/shard_map/reduce_scatter | solution.py:50
  178.1 14.3 %copy-start.4 = (bf16[2,128,2048]{2,1,0:T(8,128)(2,1)S(1)}, bf16[2,128,2048]{2,1,0:T(8,128)(2,1)}, u32[]{:S(2)}) copy-start(bf16[2,128,2048]{2,1,0:T(8,128)(2,1)} %all-gather.7.cloned.1.call-done) | copy-start | bytes 3145732
  217.2 241.4 %copy-start.1 = (bf16[128,4096]{1,0:T(8,128)(2,1)S(1)}, bf16[128,4096]{1,0:T(8,128)(2,1)}, u32[]{:S(2)}) copy-start(bf16[128,4096]{1,0:T(8,128)(2,1)} %param.3) | copy-start | bytes 3145732
Sparse Core Ops, SparseCore 0:
  22.4 34.6 reduce-scatter.2
  82.6 36.5 all-gather.4
  123.8 27.9 all-gather.8
  157.4 20.6 all-gather.6
  217.3 232.1 reduce-scatter.4
